TPU v7x, 32 devices: a whole 2x2x4 slice. The times are simulated.
32 devices in a mesh: freq: 4 (over y, x), space: 8 (over z, core).
Axes of the slice: x: 2, y: 2, z: 4, core: 2. Of those that a mesh axis runs over, the one named last changes fastest.
Arguments:
- spectra: bfloat16 [64, 24576, 256], P('freq', 'space'), may hold values from -48 to 48, as said below
- weight: float32 [24576], P('space'), may hold values from 0.25 to 4
- partner: int32 [64], P('freq'), may hold values from 0 to 15
- counts: int32 [64], P('freq'), may hold values from 1 to 8
Outputs:
- modes: bfloat16 [64, 16, 24576], P('freq', None, 'space')
- energy: float32 [64, 8], P('freq')
- coherence: float32 [64, 2, 8, 8], P('freq')
Inputs may be any that keep to these rules, and one draw needn't show every extreme that they name: spectra are finite Fourier coefficients.
All inputs are finite; a program needn't handle non-finite values.
Results may differ from a plain program's by a relative error of at most 0.0045.
Values may be sent and summed in bfloat16 or wider, within the bound.
A program may use at most 128 MiB of HBM per device.

v0:
```python
import jax
import jax.numpy as jnp
from jax import lax
from jax.sharding import PartitionSpec as P

KMAX = 8
ITERS = 4


def from_partner(block, axis, apart):
    count = lax.axis_size(axis)
    route = []
    for low in range(count):
        high = low | 1 << apart
        if high != low and high < count:
            route += [(low, high), (high, low)]
    return lax.ppermute(block, axis, route)


def embed(gram_re, gram_im):
    top = jnp.concatenate([gram_re, -gram_im], axis=2)
    bottom = jnp.concatenate([gram_im, gram_re], axis=2)
    return jnp.concatenate([top, bottom], axis=1)


def apply_operator(operator, basis):
    return jnp.einsum("fkc,fdc->fkd", basis, operator, precision=lax.Precision.HIGHEST)


def orthonormal(vectors, half):
    done = []
    for index in range(vectors.shape[1]):
        vector = vectors[:, index, :]
        for earlier in done:
            early_re, early_im = (earlier[:, :half], earlier[:, half:])
            vec_re, vec_im = (vector[:, :half], vector[:, half:])
            proj_re = jnp.sum(early_re * vec_re + early_im * vec_im, axis=1, keepdims=True)
            proj_im = jnp.sum(early_re * vec_im - early_im * vec_re, axis=1, keepdims=True)
            new_re = vec_re - proj_re * early_re + proj_im * early_im
            new_im = vec_im - proj_re * early_im - proj_im * early_re
            vector = jnp.concatenate([new_re, new_im], axis=1)
        length = jnp.sqrt(jnp.sum(vector * vector, axis=1, keepdims=True) + 1e-06)
        done.append(vector / length)
    return jnp.stack(done, axis=1)


def solve(gram_re, gram_im):
    half = gram_re.shape[1]
    operator = embed(gram_re, gram_im)
    basis = jnp.broadcast_to(
        jnp.eye(KMAX, 2 * half, dtype=jnp.float32), (gram_re.shape[0], KMAX, 2 * half)
    )
    for sweep in range(ITERS):
        basis = orthonormal(apply_operator(operator, basis), half)
    image = apply_operator(operator, basis)
    energy = jnp.sum(basis * image, axis=2)
    return (basis, energy)


def combine(moments, half, total):
    gram_re = (moments[:, :half, :half] + moments[:, half:, half:]) / total
    gram_im = (moments[:, :half, half:] - moments[:, half:, :half]) / total
    return (gram_re, gram_im)


def coefficients(basis, energy, counts):
    half = basis.shape[2] // 2
    ranks = jnp.arange(KMAX, dtype=jnp.int32)[None, :]
    scale = jnp.where(ranks < counts[:, None], 1.0 / jnp.sqrt(energy + 1e-06), 0.0)[:, :, None]
    part_re, part_im = (basis[:, :, :half], basis[:, :, half:])
    upper = jnp.concatenate([part_re, -part_im], axis=2) * scale
    lower = jnp.concatenate([part_im, part_re], axis=2) * scale
    return jnp.concatenate([upper, lower], axis=1).astype(jnp.bfloat16)


def cross_terms(own_modes, other_modes, point_weight, total):
    phi = own_modes.astype(jnp.float32)
    psi = other_modes.astype(jnp.float32)
    wphi = phi * point_weight[None, None, :]
    highest = lax.Precision.HIGHEST

    def inner(left, right):
        return jnp.einsum("fkp,flp->fkl", left, right, precision=highest)

    real_part = inner(wphi[:, :KMAX], psi[:, :KMAX]) + inner(wphi[:, KMAX:], psi[:, KMAX:])
    imag_part = inner(wphi[:, :KMAX], psi[:, KMAX:]) - inner(wphi[:, KMAX:], psi[:, :KMAX])
    return jnp.stack([real_part, imag_part], axis=1) / total


def on_device(spectra, weight, partner, counts):
    groups = spectra.shape[0]
    half = spectra.shape[2] // 2
    total = spectra.shape[1] * lax.axis_size("space")
    weighted = (weight[None, :, None] * spectra).astype(jnp.bfloat16)
    moments = lax.dot_general(
        spectra, weighted, (((1,), (1,)), ((0,), (0,))), preferred_element_type=jnp.float32
    )
    summed = lax.psum(moments, "space")
    gram_re, gram_im = combine(summed, half, total)
    basis, energy = solve(gram_re, gram_im)
    coefficient = coefficients(basis, energy, counts)
    modes = jnp.einsum(
        "fkc,fpc->fkp", coefficient, spectra, preferred_element_type=jnp.float32
    ).astype(jnp.bfloat16)
    levels = lax.axis_size("freq").bit_length() - 1
    mirrored = modes
    for bit in range(levels):
        mirrored = from_partner(mirrored, "freq", bit)
    match = (partner[:, None] == jnp.arange(groups, dtype=jnp.int32)[None, :]).astype(jnp.bfloat16)
    chosen = jnp.einsum("fg,gkp->fkp", match, mirrored, preferred_element_type=jnp.float32).astype(
        jnp.bfloat16
    )
    local = cross_terms(modes, chosen, weight, total)
    coherence = lax.psum(local, "space")
    return (modes, energy, coherence)


def solution(mesh):
    in_specs = (P("freq", "space", None), P("space"), P("freq"), P("freq"))
    out_specs = (P("freq", None, "space"), P("freq", None), P("freq", None, None, None))
    return jax.shard_map(
        on_device, mesh=mesh, in_specs=in_specs, out_specs=out_specs, check_vma=False
    )
```

profile of v0, /device:TPU:0, one launch (start us, length us, event | category | flops | bytes accessed | tf_op | source)
XLA Modules:
  0.0 290.2 jit_solution(2149110146235932898)
XLA Ops:
  7.2 20.7 %fusion.2 = f32[16,256,256]{1,2,0:T(8,128)} fusion(bf16[16,3072,256]{2,1,0:T(8,128)(2,1)} %param.4, f32[3072]{0:T(1024)} %param.5), kind=kOutput, calls=%fused_computation.7 | convolution fusion | flops 6480199680 | bytes 29372416 | tf_op jit(solution)/shard_map/dot_general | solution.py:95
  27.9 99.3 %all-reduce.2.cloned.1.call-done = f32[16,256,256]{1,2,0:T(8,128)} async-done(((f32[16,256,256]{1,2,0:T(8,128)}), f32[16,256,256]{1,2,0:T(8,128)}) %all-reduce.2.cloned.1.call-update) | async-done | bytes 4194320 | tf_op jit(solution)/shard_map/psum | solution.py:98
  127.2 2.8 fusion.80
  130.0 1.9 fusion.42
  132.7 0.3 add_reduce_fusion.96
  133.0 0.3 add_reduce_fusion.95
  133.6 0.3 add_reduce_fusion.89
  134.4 0.3 add_reduce_fusion.88
  135.1 0.3 add_reduce_fusion.87
  135.4 0.3 add_reduce_fusion.86
  136.0 0.2 add_reduce_fusion.85
  137.4 2.0 fusion.40
  140.2 0.3 add_reduce_fusion.68
  140.5 0.3 add_reduce_fusion.67
  141.1 0.3 add_reduce_fusion.61
  141.9 0.3 add_reduce_fusion.60
  142.7 0.3 add_reduce_fusion.59
  142.9 0.3 add_reduce_fusion.58
  143.5 0.2 add_reduce_fusion.57
  145.0 2.0 fusion.38
  147.8 0.3 add_reduce_fusion.40
  148.1 0.3 add_reduce_fusion.39
  148.6 0.3 add_reduce_fusion.33
  149.4 0.3 add_reduce_fusion.32
  150.2 0.3 add_reduce_fusion.31
  150.5 0.3 add_reduce_fusion.30
  151.0 0.2 add_reduce_fusion.29
  152.5 2.2 fusion.36
  155.5 0.3 add_reduce_fusion.12
  155.8 0.3 add_reduce_fusion.11
  156.4 0.3 add_reduce_fusion.5
  157.2 0.3 add_reduce_fusion.4
  157.9 0.3 add_reduce_fusion.3
  158.2 0.3 add_reduce_fusion.2
  158.8 0.2 add_reduce_fusion.1
  160.3 2.0 fusion.34
  162.5 12.4 %convert_multiply_fusion = (f32[16,16,3072]{2,1,0:T(8,128)S(1)}, bf16[16,16,3072]{2,1,0:T(8,128)(2,1)}) fusion(f32[3072]{0:T(1024)S(1)} %copy-done, bf16[16,3072,256]{2,1,0:T(8,128)(2,1)} %param.4, bf16[16,16,256]{2,0,1:T(8,128)(2,1)S(1)} %pad_maximum_fusion), kind=kOutput, calls=%fused_computation.6 | convolution fusion | flops 405012480 | bytes 30027776 | tf_op jit(solution)/shard_map/fkc,fpc->fkp/dot_general | solution.py:102
  175.0 1.5 collective-permute-start
  176.5 34.6 %collective-permute-done = bf16[16,16,3072]{2,1,0:T(8,128)(2,1)S(1)} collective-permute-done((bf16[16,16,3072]{2,1,0:T(8,128)(2,1)}, bf16[16,16,3072]{2,1,0:T(8,128)(2,1)S(1)}, u32[]{:S(2)}, u32[]{:S(2)}) %collective-permute-start) | collective-permute-done | bytes 1572896 | tf_op jit(solution)/shard_map/ppermute | solution.py:17
  211.1 1.5 collective-permute-start.1
  212.6 33.6 %collective-permute-done.1 = bf16[16,16,3072]{2,1,0:T(8,128)(2,1)S(1)} collective-permute-done((bf16[16,16,3072]{2,1,0:T(8,128)(2,1)S(1)}, bf16[16,16,3072]{2,1,0:T(8,128)(2,1)S(1)}, u32[]{:S(2)}, u32[]{:S(2)}) %collective-permute-start.1) | collective-permute-done | bytes 1572896 | tf_op jit(solution)/shard_map/ppermute | solution.py:17
  246.1 1.9 convolution_convert_fusion
  248.1 1.8 fusion.6
  249.9 1.8 fusion.4
  251.7 1.5 fusion.15
  253.2 1.8 fusion.21
  255.0 27.5 %psum.15 = f32[16,2,8,8]{3,2,0,1:T(8,128)S(1)} all-reduce(f32[16,2,8,8]{3,2,0,1:T(8,128)S(1)} %maximum_multiply_fusion.2), channel_id=1, replica_groups=mesh['freq'=4,'space'=8] {'space'}, use_global_device_ids=true, to_apply=%region_258.259 | all-reduce | flops 2048 | bytes 16384 | tf_op jit(solution)/shard_map/psum | solution.py:114
  282.6 0.7 copy.52
  (215 shorter events, 14.6 us)
Async XLA Ops:
  7.2 120.1 %all-reduce.2.cloned.1.call-start = ((), (), s32[]{:S(2)}) async-start(), calls=%async_computation | async-start | bytes 8388608 | tf_op jit(solution)/shard_map/psum | solution.py:98
  158.5 3.9 %copy-start.2 = (s32[16]{0:T(128)S(1)}, s32[16]{0:T(128)}, u32[]{:S(2)}) copy-start(s32[16]{0:T(128)} %param.7) | copy-start | bytes 196
  160.0 2.6 copy-start
  162.4 12.6 %copy-start.1 = (f32[16,8]{0,1:T(8,128)}, f32[16,8]{0,1:T(8,128)S(1)}, u32[]{:S(2)}) copy-start(f32[16,8]{0,1:T(8,128)S(1)} %fusion.33) | copy-start | bytes 1540
  162.5 83.6 %copy-start.3 = (s32[16]{0:T(128)S(1)}, s32[16]{0:T(128)}, u32[]{:S(2)}) copy-start(s32[16]{0:T(128)} %param.6) | copy-start | bytes 196
  175.0 36.1 %collective-permute-start = (bf16[16,16,3072]{2,1,0:T(8,128)(2,1)}, bf16[16,16,3072]{2,1,0:T(8,128)(2,1)S(1)}, u32[]{:S(2)}, u32[]{:S(2)}) collective-permute-start(bf16[16,16,3072]{2,1,0:T(8,128)(2,1)} %get-tuple-element.649), channel_id=1, source_target_pairs={{0,8},{8,0},{16,24},{24,16},{1,9},{9,1},{17,25},{25,17},{2,10},{10... | collective-permute-start | bytes 4718600 | tf_op jit(solution)/shard_map/ppermute | solution.py:17
  211.1 35.0 %collective-permute-start.1 = (bf16[16,16,3072]{2,1,0:T(8,128)(2,1)S(1)}, bf16[16,16,3072]{2,1,0:T(8,128)(2,1)S(1)}, u32[]{:S(2)}, u32[]{:S(2)}) collective-permute-start(bf16[16,16,3072]{2,1,0:T(8,128)(2,1)S(1)} %collective-permute-done), channel_id=1, source_target_pairs={{0,16},{16,0},{8,24},{24,8},{1,17},{17,1},{9,25},{25,9},{2,18},{18... | collective-permute-start | bytes 4718600 | tf_op jit(solution)/shard_map/ppermute | solution.py:17
Sparse Core Ops, SparseCore 0:
  28.0 99.1 all-reduce.1
where the time goes:
time: 290 us
  waiting for transfers between devices  168 us (58%)
  matrix products  51.8 us (18%)
  blocking collectives  27.5 us (9%)
  other arithmetic  24.4 us (8%)
  between operations  14.6 us (5%)
  starting transfers between devices  2.98 us (1%)
    psum x1, waiting for transfers between devices, on_device(): summed = lax.psum(moments, 'space')  99.3 us
    ppermute x2, waiting for transfers between devices, from_partner(): return lax.ppermute(block, axis, route)  68.2 us
    psum x1, blocking collectives, on_device(): coherence = lax.psum(local, 'space')  27.5 us
    dot_general x1, matrix products, on_device(): lax.dot_general(spectra, weighted, (((1,), (1,)), ((0,), (0,))), preferre...  20.7 us
    dot_general x1, matrix products, on_device(): jnp.einsum('fkc,fpc->fkp', coefficient, spectra, preferred_element_type=j...  12.4 us
    reduce_sum x44, other arithmetic, orthonormal(): jnp.sum(early_re * vec_re + early_im * vec_im, axis=1, keepdims=True)  10.6 us
    dot_general x5, matrix products, apply_operator(): jnp.einsum('fkc,fdc->fkd', basis, operator, precision=lax.Precision.HIGHEST)  9.94 us
    dot_general x4, matrix products, inner(): return jnp.einsum('fkp,flp->fkl', left, right, precision=highest)  6.86 us
  transfers between devices with their start and end apart: 3, of which 3 were waited for; matrix products, arithmetic and copies ran while one was open for 0% of the time, Pallas kernels for 0%

commit v1 on v0

--- a/solution.py
+++ b/solution.py
@@ -111,7 +111,7 @@
         jnp.bfloat16
     )
     local = cross_terms(modes, chosen, weight, total)
-    coherence = lax.psum(local, "space")
+    coherence = jnp.sum(lax.all_gather(local, "space"), axis=0)
     return (modes, energy, coherence)
 
 

time: 290 us -> 278 us (0.959)
  blocking collectives: 27.5 us -> 14.9 us
    psum x1 -> x0, blocking collectives: 27.5 us -> none  [on_device(): coherence = lax.psum(local, 'space')]
    all_gather x0 -> x1, blocking collectives: none -> 14.9 us  [on_device(): coherence = jnp.sum(lax.all_gather(local, 'space'), axis=0)]
where the time goes in v1:
time: 278 us
  waiting for transfers between devices  168 us (60%)
  matrix products  52 us (19%)
  other arithmetic  25.1 us (9%)
  blocking collectives  14.9 us (5%)
  between operations  14.6 us (5%)
  starting transfers between devices  2.98 us (1%)
    psum x1, waiting for transfers between devices, on_device(): summed = lax.psum(moments, 'space')  99.3 us
    ppermute x2, waiting for transfers between devices, from_partner(): return lax.ppermute(block, axis, route)  68.2 us
    dot_general x1, matrix products, on_device(): lax.dot_general(spectra, weighted, (((1,), (1,)), ((0,), (0,))), preferre...  20.7 us
    all_gather x1, blocking collectives, on_device(): coherence = jnp.sum(lax.all_gather(local, 'space'), axis=0)  14.9 us
    dot_general x1, matrix products, on_device(): jnp.einsum('fkc,fpc->fkp', coefficient, spectra, preferred_element_type=j...  12.4 us
    reduce_sum x44, other arithmetic, orthonormal(): jnp.sum(early_re * vec_re + early_im * vec_im, axis=1, keepdims=True)  10.6 us
    dot_general x5, matrix products, apply_operator(): jnp.einsum('fkc,fdc->fkd', basis, operator, precision=lax.Precision.HIGHEST)  9.94 us
    dot_general x4, matrix products, inner(): return jnp.einsum('fkp,flp->fkl', left, right, precision=highest)  7.15 us
  transfers between devices with their start and end apart: 3, of which 3 were waited for; matrix products, arithmetic and copies ran while one was open for 0% of the time, Pallas kernels for 0%

profile of v1, /device:TPU:0, one launch (start us, length us, event | category | flops | bytes accessed | tf_op | source)
XLA Modules:
  0.0 278.1 jit_solution(5551145469311354213)
XLA Ops:
  7.2 20.7 %fusion.2 = f32[16,256,256]{1,2,0:T(8,128)} fusion(bf16[16,3072,256]{2,1,0:T(8,128)(2,1)} %param.4, f32[3072]{0:T(1024)} %param.5), kind=kOutput, calls=%fused_computation.7 | convolution fusion | flops 6480199680 | bytes 29372416 | tf_op jit(solution)/shard_map/dot_general | solution.py:95
  27.9 99.3 %all-reduce.2.cloned.1.call-done = f32[16,256,256]{1,2,0:T(8,128)} async-done(((f32[16,256,256]{1,2,0:T(8,128)}), f32[16,256,256]{1,2,0:T(8,128)}) %all-reduce.2.cloned.1.call-update) | async-done | bytes 4194320 | tf_op jit(solution)/shard_map/psum | solution.py:98
  127.2 2.8 fusion.68
  130.0 1.9 fusion.30
  132.7 0.3 add_reduce_fusion.96
  133.0 0.3 add_reduce_fusion.95
  133.6 0.3 add_reduce_fusion.89
  134.4 0.3 add_reduce_fusion.88
  135.1 0.3 add_reduce_fusion.87
  135.4 0.3 add_reduce_fusion.86
  136.0 0.2 add_reduce_fusion.85
  137.4 2.0 fusion.28
  140.2 0.3 add_reduce_fusion.68
  140.5 0.3 add_reduce_fusion.67
  141.1 0.3 add_reduce_fusion.61
  141.9 0.3 add_reduce_fusion.60
  142.7 0.3 add_reduce_fusion.59
  142.9 0.3 add_reduce_fusion.58
  143.5 0.2 add_reduce_fusion.57
  145.0 2.0 fusion.26
  147.8 0.3 add_reduce_fusion.40
  148.1 0.3 add_reduce_fusion.39
  148.6 0.3 add_reduce_fusion.33
  149.4 0.3 add_reduce_fusion.32
  150.2 0.3 add_reduce_fusion.31
  150.5 0.3 add_reduce_fusion.30
  151.0 0.2 add_reduce_fusion.29
  152.5 2.2 fusion.24
  155.5 0.3 add_reduce_fusion.12
  155.8 0.3 add_reduce_fusion.11
  156.4 0.3 add_reduce_fusion.5
  157.2 0.3 add_reduce_fusion.4
  157.9 0.3 add_reduce_fusion.3
  158.2 0.3 add_reduce_fusion.2
  158.8 0.2 add_reduce_fusion.1
  160.3 2.0 fusion.22
  162.5 12.4 %convert_multiply_fusion = (f32[16,16,3072]{2,1,0:T(8,128)S(1)}, bf16[16,16,3072]{2,1,0:T(8,128)(2,1)}) fusion(f32[3072]{0:T(1024)S(1)} %copy-done, bf16[16,3072,256]{2,1,0:T(8,128)(2,1)} %param.4, bf16[16,16,256]{2,0,1:T(8,128)(2,1)S(1)} %pad_maximum_fusion), kind=kOutput, calls=%fused_computation.6 | convolution fusion | flops 405012480 | bytes 30027776 | tf_op jit(solution)/shard_map/fkc,fpc->fkp/dot_general | solution.py:102
  175.0 1.5 collective-permute-start
  176.5 34.6 %collective-permute-done = bf16[16,16,3072]{2,1,0:T(8,128)(2,1)S(1)} collective-permute-done((bf16[16,16,3072]{2,1,0:T(8,128)(2,1)}, bf16[16,16,3072]{2,1,0:T(8,128)(2,1)S(1)}, u32[]{:S(2)}, u32[]{:S(2)}) %collective-permute-start) | collective-permute-done | bytes 1572896 | tf_op jit(solution)/shard_map/ppermute | solution.py:17
  211.1 1.5 collective-permute-start.1
  212.6 33.6 %collective-permute-done.1 = bf16[16,16,3072]{2,1,0:T(8,128)(2,1)S(1)} collective-permute-done((bf16[16,16,3072]{2,1,0:T(8,128)(2,1)S(1)}, bf16[16,16,3072]{2,1,0:T(8,128)(2,1)S(1)}, u32[]{:S(2)}, u32[]{:S(2)}) %collective-permute-start.1) | collective-permute-done | bytes 1572896 | tf_op jit(solution)/shard_map/ppermute | solution.py:17
  246.1 1.9 convolution_convert_fusion
  248.1 1.8 fusion.10
  249.9 1.8 fusion.4
  251.7 1.8 fusion.6
  253.5 1.8 fusion.8
  255.7 14.9 %all_gather.4 = f32[8,16,2,8,8]{1,4,3,2,0:T(8,128)S(1)} all-gather(f32[1,16,2,8,8]{1,4,3,2,0:T(8,128)S(1)} %maximum_multiply_fusion.2), channel_id=1, replica_groups=mesh['freq'=4,'space'=8] {'space'}, dimensions={0}, use_global_device_ids=true | all-gather | bytes 73728 | tf_op jit(solution)/shard_map/all_gather | solution.py:114
  270.6 0.7 reduce_sum.2579
  (221 shorter events, 15.0 us)
Async XLA Ops:
  7.2 120.1 %all-reduce.2.cloned.1.call-start = ((), (), s32[]{:S(2)}) async-start(), calls=%async_computation | async-start | bytes 8388608 | tf_op jit(solution)/shard_map/psum | solution.py:98
  158.5 3.9 %copy-start.2 = (s32[16]{0:T(128)S(1)}, s32[16]{0:T(128)}, u32[]{:S(2)}) copy-start(s32[16]{0:T(128)} %param.7) | copy-start | bytes 196
  160.0 2.6 copy-start
  162.4 12.6 %copy-start.1 = (f32[16,8]{0,1:T(8,128)}, f32[16,8]{0,1:T(8,128)S(1)}, u32[]{:S(2)}) copy-start(f32[16,8]{0,1:T(8,128)S(1)} %fusion.21) | copy-start | bytes 1540
  162.5 83.6 %copy-start.3 = (s32[16]{0:T(128)S(1)}, s32[16]{0:T(128)}, u32[]{:S(2)}) copy-start(s32[16]{0:T(128)} %param.6) | copy-start | bytes 196
  175.0 36.1 %collective-permute-start = (bf16[16,16,3072]{2,1,0:T(8,128)(2,1)}, bf16[16,16,3072]{2,1,0:T(8,128)(2,1)S(1)}, u32[]{:S(2)}, u32[]{:S(2)}) collective-permute-start(bf16[16,16,3072]{2,1,0:T(8,128)(2,1)} %get-tuple-element.652), channel_id=1, source_target_pairs={{0,8},{8,0},{16,24},{24,16},{1,9},{9,1},{17,25},{25,17},{2,10},{10... | collective-permute-start | bytes 4718600 | tf_op jit(solution)/shard_map/ppermute | solution.py:17
  211.1 35.0 %collective-permute-start.1 = (bf16[16,16,3072]{2,1,0:T(8,128)(2,1)S(1)}, bf16[16,16,3072]{2,1,0:T(8,128)(2,1)S(1)}, u32[]{:S(2)}, u32[]{:S(2)}) collective-permute-start(bf16[16,16,3072]{2,1,0:T(8,128)(2,1)S(1)} %collective-permute-done), channel_id=1, source_target_pairs={{0,16},{16,0},{8,24},{24,8},{1,17},{17,1},{9,25},{25,9},{2,18},{18... | collective-permute-start | bytes 4718600 | tf_op jit(solution)/shard_map/ppermute | solution.py:17
Sparse Core Ops, SparseCore 0:
  28.0 99.1 all-reduce.1
